TPU v7x, 32 devices: a whole 2x2x4 slice. The times are simulated.
32 devices in a mesh: pipe: 4 (over z), dp: 4 (over y, x), tensor: 2 (over core).
Axes of the slice: x: 2, y: 2, z: 4, core: 2. Of those that a mesh axis runs over, the one named last changes fastest.
Arguments:
- saved_inputs: bfloat16 [3, 2, 4, 512, 4096], P(None, None, 'pipe', 'dp', 'tensor'), may hold values from -6 to 6
- proj_in: bfloat16 [2, 4, 512, 4096], P(None, 'pipe', None, 'tensor'), may hold values from -0.09375 to 0.09375
- proj_out: bfloat16 [2, 4, 512, 4096], P(None, 'pipe', None, 'tensor'), may hold values from -0.25 to 0.25
- norm_gain: float32 [2, 4, 4096], P(None, 'pipe', 'tensor'), may hold values from 0.1 to 1.9
- arriving: bfloat16 [2, 4, 512, 4096], P(None, 'pipe', 'dp', 'tensor'), may hold values from -6 to 6
- logp_grad: bfloat16 [2, 512, 4096], P(None, 'dp', 'tensor'), may hold values from -6 to 6
- rewards: float32 [2, 4, 4], P(None, 'dp'), may hold values from -4 to 4
- seq_lengths: int32 [2, 4, 4], P(None, 'dp'), may hold values from 1 to 64, 128 in all within a row
- group_ids: int32 [2, 4, 4], P(None, 'dp'), may hold values from 0 to 3
Outputs:
- grad_in: float32 [2, 4, 512, 4096], P(None, 'pipe', 'dp', 'tensor')
- grad_out: float32 [2, 4, 512, 4096], P(None, 'pipe', 'dp', 'tensor')
- leaving: bfloat16 [2, 4, 512, 4096], P(None, 'pipe', 'dp', 'tensor')
Inputs may be any that keep to these rules, and one draw needn't show every extreme that they name: `seq_lengths`: the 4 lengths of one microbatch on one replica sum to 128. `group_ids`: groups take sequences from several replicas and microbatches.
All inputs are finite; a program needn't handle non-finite values.
Results may differ from a plain program's by a relative error of at most 0.023.
Values may be sent and summed in bfloat16 or wider, within the bound.
A program may use at most 128 MiB of HBM per device.

v0:
```python
import jax
import jax.numpy as jnp
from jax import lax
from jax.sharding import PartitionSpec as P

D = 4096


EPS = 1e-05


def shifted(x, axis, by):
    count = lax.axis_size(axis)
    return lax.ppermute(x, axis, [(i, (i + by) % count) for i in range(count)])


def silu_slope(values):
    sigma = jax.nn.sigmoid(values)
    return sigma * (1.0 + values * (1.0 - sigma))


def block_back(inputs, arrive, weight_in, weight_out, gain_rows, inv_rms):
    inputs_f = inputs.astype(jnp.float32)
    gained = (inputs_f * gain_rows[:, None, :]).astype(jnp.bfloat16)
    part_pre = jnp.einsum("vrd,vkd->vrk", gained, weight_in, preferred_element_type=jnp.float32)
    part_back = jnp.einsum("vrd,vkd->vrk", arrive, weight_out, preferred_element_type=jnp.float32)
    pre_sum, back_sum = (
        lax.psum(part_pre.astype(jnp.bfloat16), "tensor").astype(jnp.float32),
        lax.psum(part_back.astype(jnp.bfloat16), "tensor").astype(jnp.float32),
    )
    scaled = inv_rms[..., None]
    pre_act = scaled * pre_sum
    hidden = jax.nn.silu(pre_act).astype(jnp.bfloat16)
    grad_pre = back_sum * silu_slope(pre_act)
    grad_scaled = (scaled * grad_pre).astype(jnp.bfloat16)
    term_in = jnp.einsum("vrk,vrd->vkd", grad_scaled, gained, preferred_element_type=jnp.float32)
    term_out = jnp.einsum("vrk,vrd->vkd", hidden, arrive, preferred_element_type=jnp.float32)
    grad_gained = jnp.einsum(
        "vrk,vkd->vrd", grad_scaled, weight_in, preferred_element_type=jnp.float32
    )
    radial_sum = jnp.sum(grad_pre * pre_sum, axis=-1)
    out_cot = (
        arrive.astype(jnp.float32)
        + gain_rows[:, None, :] * grad_gained
        - inputs_f * (inv_rms**3 * radial_sum / D)[..., None]
    )
    return (out_cot.astype(jnp.bfloat16), term_in, term_out)


def shards(
    saved_inputs, proj_in, proj_out, norm_gain, arriving, logp_grad, rewards, seq_lengths, group_ids
):
    sections = lax.axis_size("pipe")
    section = lax.axis_index("pipe")
    replicas = lax.axis_size("dp")
    saved = saved_inputs[:, :, 0]
    weights_in = proj_in[:, 0]
    weights_out = proj_out[:, 0]
    gains = norm_gain[:, 0]
    current = arriving[:, 0]
    step_count = saved.shape[0]
    local_rows = saved.shape[2]
    new_count = logp_grad.shape[0]
    seq_count = rewards.shape[2]
    group_count = new_count * replicas * seq_count // 8
    saved_f = saved.astype(jnp.float32)
    squares = jnp.sum(saved_f * saved_f, axis=-1)
    totals = lax.psum(squares, "tensor")
    inv_rms_all = 1.0 / jnp.sqrt(totals / D + EPS)
    groups = jnp.arange(group_count, dtype=jnp.int32)
    member = (group_ids[..., None] == groups).astype(jnp.float32)
    sums = jnp.sum(member * rewards[..., None], axis=(0, 1, 2))
    counts = jnp.sum(member, axis=(0, 1, 2))
    sums, counts = lax.psum((sums, counts), "dp")
    means = sums / jnp.maximum(counts, 1.0)
    advantage = rewards - jnp.sum(member * means, axis=-1)
    ends = jnp.cumsum(seq_lengths, axis=-1)
    position = jnp.arange(local_rows, dtype=jnp.int32)
    segment = jnp.sum((position[:, None] >= ends[..., None, :]).astype(jnp.int32), axis=-1)
    pick = (segment[..., None] == jnp.arange(seq_count, dtype=jnp.int32)).astype(jnp.float32)
    token_weight = jnp.sum(pick * advantage[..., None, :], axis=-1)[:, 0]
    entering = (-token_weight[..., None] * logp_grad.astype(jnp.float32)).astype(jnp.bfloat16)

    def run_blocks(first, last, arrive, step_index):
        return block_back(
            saved[step_index, first:last],
            arrive,
            weights_in,
            weights_out,
            gains,
            inv_rms_all[step_index, first:last],
        )

    is_top = section == sections - 1
    acc_in = jnp.zeros((2,) + weights_in.shape[1:], jnp.float32)
    acc_out = jnp.zeros((2,) + weights_in.shape[1:], jnp.float32)
    for step_index in range(step_count - 1):
        moved, add_in, add_out = run_blocks(0, 2, current, step_index)
        acc_in = acc_in + add_in
        acc_out = acc_out + add_out
        received = shifted(moved, "pipe", -1)
        from_upper = received[1]
        from_lower = received[0]
        upper_next = jnp.where(is_top, entering[step_index], from_upper)
        lower_next = jnp.where(is_top, from_upper, from_lower)
        current = jnp.stack([lower_next, upper_next])
    final_index = step_count - 1
    leaving, add_in, add_out = run_blocks(0, 2, current, final_index)
    summed_in, summed_out = (
        lax.psum_scatter(
            (acc_in + add_in).astype(jnp.bfloat16), "dp", scatter_dimension=1, tiled=True
        ).astype(jnp.float32),
        lax.psum_scatter(
            (acc_out + add_out).astype(jnp.bfloat16), "dp", scatter_dimension=1, tiled=True
        ).astype(jnp.float32),
    )
    scale = 1.0 / (replicas * local_rows)
    return ((summed_in * scale)[:, None], (summed_out * scale)[:, None], leaving[:, None])


def solution(mesh):
    return jax.shard_map(
        shards,
        mesh=mesh,
        in_specs=(
            P(None, None, "pipe", "dp", "tensor"),
            P(None, "pipe", None, "tensor"),
            P(None, "pipe", None, "tensor"),
            P(None, "pipe", "tensor"),
            P(None, "pipe", "dp", "tensor"),
            P(None, "dp", "tensor"),
            P(None, "dp", None),
            P(None, "dp", None),
            P(None, "dp", None),
        ),
        out_specs=(
            P(None, "pipe", "dp", "tensor"),
            P(None, "pipe", "dp", "tensor"),
            P(None, "pipe", "dp", "tensor"),
        ),
        check_vma=False,
    )
```

profile of v0, /device:TPU:0, one launch (start us, length us, event | category | flops | bytes accessed | tf_op | source)
XLA Modules:
  0.0 281.6 jit_solution(14688957267595545626)
XLA Ops:
  8.1 4.8 %fusion.43 = bf16[2,128,512]{2,1,0:T(8,128)(2,1)} fusion(bf16[2,1,512,2048]{3,2,1,0:T(8,128)(2,1)} %param.11, bf16[2,1,128,2048]{3,2,1,0:T(8,128)(2,1)} %param.13), kind=kOutput, calls=%fused_computation.43 | convolution fusion | flops 537001984 | bytes 5505024 | tf_op jit(solution)/shard_map/vrd,vkd->vrk/dot_general | solution.py:26
  12.9 4.4 %fusion.52 = bf16[2,128,512]{2,1,0:T(8,128)(2,1)} fusion(bf16[2,1,512,2048]{3,2,1,0:T(8,128)(2,1)} %param.10, f32[2,2048]{1,0:T(2,128)S(1)} %bitcast.130, bf16[3,2,1,128,2048]{4,3,1,2,0:T(8,128)(2,1)S(1)} %bitcast.121), kind=kOutput, calls=%fused_computation.46 | convolution fusion | flops 538574848 | bytes 5521408 | tf_op jit(solution)/shard_map/vrd,vkd->vrk/dot_general | solution.py:25
  18.2 11.4 %all-reduce = (f32[4]{0:T(128)S(1)}, f32[4]{0:T(128)S(1)}) all-reduce(f32[4]{0:T(128)S(1)} %get-tuple-element.10, f32[4]{0:T(128)S(1)} %get-tuple-element.9), channel_id=1, replica_groups=mesh['pipe'=4,'dp'=4,'tensor'=2] {'dp'}, use_global_device_ids=true, to_apply=%region_8.9 | all-reduce | flops 8 | bytes 64 | tf_op jit(solution)/shard_map/psum | solution.py:74
  29.9 2.4 psum.63
  32.4 6.5 %all-reduce.12.cloned.1.call-done = (bf16[2,128,512]{2,1,0:T(8,128)(2,1)}, bf16[2,128,512]{2,1,0:T(8,128)(2,1)}) async-done(((bf16[2,128,512]{2,1,0:T(8,128)(2,1)}, bf16[2,128,512]{2,1,0:T(8,128)(2,1)}), (bf16[2,128,512]{2,1,0:T(8,128)(2,1)}, bf16[2,128,512]{2,1,0:T(8,128)(2,1)})) %all-reduce.12.cloned.1.call-update) | async-done | bytes 524304 | tf_op jit(solution)/shard_map/psum | solution.py:28
  40.3 5.0 %fusion.33 = bf16[2,128,2048]{2,1,0:T(8,128)(2,1)} fusion(bf16[2,1,512,2048]{3,2,1,0:T(8,128)(2,1)} %param.10, bf16[2,1,128,2048]{3,2,1,0:T(8,128)(2,1)} %param.13, f32[2,128]{1,0:T(2,128)S(1)} %fusion.121, f32[2,2048]{1,0:T(2,128)S(1)} %bitcast.131, bf16[3,2,1,128,2048]{4,3,1,2,0:T(8,128)(2,1)S(1)} %bitcast.122, f32[2,128]{1,0:T(2,128)S(1)} %get-tuple-element.25, ...), kind=kOutput, calls=%fused_computation.32 | convolution fusion | flops 542244864 | bytes 7882752 | tf_op jit(solution)/shard_map/vrk,vkd->vrd/dot_general | solution.py:38
  45.3 3.6 %collective-permute-start = (bf16[2,128,2048]{2,1,0:T(8,128)(2,1)}, bf16[2,128,2048]{2,1,0:T(8,128)(2,1)}, u32[]{:S(2)}, u32[]{:S(2)}) collective-permute-start(bf16[2,128,2048]{2,1,0:T(8,128)(2,1)} %fusion.33), channel_id=1, source_target_pairs={{0,24},{8,0},{16,8},{24,16},{1,25},{9,1},{17,9},{25,17},{2,26},{10... | collective-permute-start | bytes 3145736 | tf_op jit(solution)/shard_map/ppermute | solution.py:14
  49.1 4.5 %fusion.55 = bf16[2,128,512]{2,1,0:T(8,128)(2,1)} fusion(bf16[2,1,512,2048]{3,2,1,0:T(8,128)(2,1)} %param.10, f32[2,2048]{1,0:T(2,128)S(1)} %bitcast.132, bf16[3,2,1,128,2048]{4,3,1,2,0:T(8,128)(2,1)S(1)} %bitcast.123), kind=kOutput, calls=%fused_computation.47 | convolution fusion | flops 538574848 | bytes 5521408 | tf_op jit(solution)/shard_map/vrd,vkd->vrk/dot_general | solution.py:25
  53.9 18.2 %collective-permute-done = bf16[2,128,2048]{2,1,0:T(8,128)(2,1)} collective-permute-done((bf16[2,128,2048]{2,1,0:T(8,128)(2,1)}, bf16[2,128,2048]{2,1,0:T(8,128)(2,1)}, u32[]{:S(2)}, u32[]{:S(2)}) %collective-permute-start) | collective-permute-done | bytes 1048608 | tf_op jit(solution)/shard_map/ppermute | solution.py:14
  76.6 20.6 %all-reduce.10.cloned.1.call-done = (bf16[2,128,512]{2,1,0:T(8,128)(2,1)}, bf16[2,128,512]{2,1,0:T(8,128)(2,1)}) async-done(((bf16[2,128,512]{2,1,0:T(8,128)(2,1)}, bf16[2,128,512]{2,1,0:T(8,128)(2,1)}), (bf16[2,128,512]{2,1,0:T(8,128)(2,1)}, bf16[2,128,512]{2,1,0:T(8,128)(2,1)})) %all-reduce.10.cloned.1.call-update) | async-done | bytes 524304 | tf_op jit(solution)/shard_map/psum | solution.py:28
  98.7 4.1 %fusion.39 = bf16[2,128,2048]{2,1,0:T(8,128)(2,1)S(1)} fusion(f32[2,128]{1,0:T(2,128)S(1)} %fusion.123, bf16[2,1,512,2048]{3,2,1,0:T(8,128)(2,1)} %param.10, f32[2,2048]{1,0:T(2,128)S(1)} %bitcast.133, bf16[3,2,1,128,2048]{4,3,1,2,0:T(8,128)(2,1)S(1)} %bitcast.124, bf16[1,128,2048]{2,1,0:T(8,128)(2,1)} %copy-done.13, bf16[1,128,2048]{2,1,0:T(8,128)(2,1)} %copy-done.11, ...), kind=kOutput, calls=%fused_computation.36 | convolution fusion | flops 542769152 | bytes 7882752 | tf_op jit(solution)/shard_map/vrk,vkd->vrd/dot_general | solution.py:38
  102.8 3.7 %collective-permute-start.1 = (bf16[2,128,2048]{2,1,0:T(8,128)(2,1)S(1)}, bf16[2,128,2048]{2,1,0:T(8,128)(2,1)S(1)}, u32[]{:S(2)}, u32[]{:S(2)}) collective-permute-start(bf16[2,128,2048]{2,1,0:T(8,128)(2,1)S(1)} %fusion.39), channel_id=1, source_target_pairs={{0,24},{8,0},{16,8},{24,16},{1,25},{9,1},{17,9},{25,17},{2,26},{10... | collective-permute-start | bytes 3145736 | tf_op jit(solution)/shard_map/ppermute | solution.py:14
  108.7 20.6 %collective-permute-done.1 = bf16[2,128,2048]{2,1,0:T(8,128)(2,1)S(1)} collective-permute-done((bf16[2,128,2048]{2,1,0:T(8,128)(2,1)S(1)}, bf16[2,128,2048]{2,1,0:T(8,128)(2,1)S(1)}, u32[]{:S(2)}, u32[]{:S(2)}) %collective-permute-start.1) | collective-permute-done | bytes 1048608 | tf_op jit(solution)/shard_map/ppermute | solution.py:14
  132.9 5.9 %fusion.62 = f32[2,512,2048]{2,1,0:T(8,128)} fusion(bf16[2,1,128,2048]{3,2,1,0:T(8,128)(2,1)} %param.13, bf16[2,128,512]{2,1,0:T(8,128)(2,1)S(1)} %copy-done.6, f32[2,128]{1,0:T(2,128)S(1)} %get-tuple-element.25), kind=kOutput, calls=%fused_computation.55 | convolution fusion | flops 537788416 | bytes 9700352 | tf_op jit(solution)/shard_map/vrk,vrd->vkd/dot_general | solution.py:37
  138.9 4.6 %fusion.110 = f32[2,512,2048]{2,1,0:T(8,128)} fusion(bf16[1,128,2048]{2,1,0:T(8,128)(2,1)S(1)} %copy-done.14, bf16[1,128,2048]{2,1,0:T(8,128)(2,1)S(1)} %copy-done.12, bf16[2,128,512]{2,1,0:T(8,128)(2,1)S(1)} %copy-done.7, f32[2,128]{1,0:T(2,128)S(1)} %get-tuple-element.24), kind=kOutput, calls=%fused_computation.106 | convolution fusion | flops 538312704 | bytes 9700352 | tf_op jit(solution)/shard_map/vrk,vrd->vkd/dot_general | solution.py:37
  143.4 9.9 %all-reduce.8.cloned.1.call-done = (bf16[2,128,512]{2,1,0:T(8,128)(2,1)}, bf16[2,128,512]{2,1,0:T(8,128)(2,1)}) async-done(((bf16[2,128,512]{2,1,0:T(8,128)(2,1)}, bf16[2,128,512]{2,1,0:T(8,128)(2,1)}), (bf16[2,128,512]{2,1,0:T(8,128)(2,1)}, bf16[2,128,512]{2,1,0:T(8,128)(2,1)})) %all-reduce.8.cloned.1.call-update) | async-done | bytes 524304 | tf_op jit(solution)/shard_map/psum | solution.py:28
  153.3 9.5 %add_convert_fusion = bf16[2,512,2048]{2,1,0:T(8,128)(2,1)} fusion(f32[2,512,2048]{2,1,0:T(8,128)} %fusion.62, f32[2,512,2048]{2,1,0:T(8,128)} %fusion.110, bf16[1,128,2048]{2,1,0:T(8,128)(2,1)} %copy-done.10, bf16[1,128,2048]{2,1,0:T(8,128)(2,1)} %copy-done.9, bf16[2,128,512]{2,1,0:T(8,128)(2,1)} %get-tuple-element.13, f32[2,128]{1,0:T(2,128)S(1)} %get-tuple-element.23), kind=kOutput, calls=%fused_computation | convolution fusion | flops 544604160 | bytes 22283264 | tf_op jit(solution)/shard_map/vrk,vrd->vkd/dot_general | solution.py:37
  162.9 2.4 fusion.74
  166.9 3.7 %add_convert_fusion.1 = bf16[2,512,2048]{2,1,0:T(8,128)(2,1)} fusion(f32[2,512,2048]{2,1,0:T(8,128)S(1)} %fusion.74, f32[2,512,2048]{2,1,0:T(8,128)S(1)} %fusion.71, f32[2,2048]{1,0:T(2,128)S(1)} %bitcast.137, bf16[3,2,1,128,2048]{4,3,1,2,0:T(8,128)(2,1)S(1)} %bitcast.128, f32[2,128]{1,0:T(2,128)S(1)} %get-tuple-element.23, ...), kind=kOutput, calls=%fused_computation.1 | convolution fusion | flops 546439168 | bytes 22561792 | tf_op jit(solution)/shard_map/vrk,vrd->vkd/dot_general | solution.py:36
  172.0 4.8 %fusion.61 = bf16[2,1,128,2048]{3,2,1,0:T(8,128)(2,1)} fusion(f32[2,128]{1,0:T(2,128)S(1)} %fusion.125, bf16[2,1,512,2048]{3,2,1,0:T(8,128)(2,1)} %param.10, f32[2,2048]{1,0:T(2,128)S(1)} %bitcast.138, bf16[3,2,1,128,2048]{4,3,1,2,0:T(8,128)(2,1)S(1)} %bitcast.129, bf16[1,128,2048]{2,1,0:T(8,128)(2,1)} %copy-done.10, bf16[1,128,2048]{2,1,0:T(8,128)(2,1)} %copy-done.9, ...), kind=kOutput, calls=%fused_computation.49 | convolution fusion | flops 542769152 | bytes 7882752 | tf_op jit(solution)/shard_map/vrk,vkd->vrd/dot_general | solution.py:38
  176.9 40.0 %reduce-scatter.5.cloned.1.call-done = bf16[2,128,2048]{2,1,0:T(8,128)(2,1)} async-done(((bf16[2,512,2048]{2,1,0:T(8,128)(2,1)}), bf16[2,128,2048]{2,1,0:T(8,128)(2,1)}) %reduce-scatter.5.cloned.1.call-update) | async-done | bytes 1048592 | tf_op jit(solution)/shard_map/reduce_scatter | solution.py:113
  216.8 2.8 multiply_bitcast_fusion
  219.6 52.7 %reduce-scatter.3.cloned.1.call-done = bf16[2,128,2048]{2,1,0:T(8,128)(2,1)} async-done(((bf16[2,512,2048]{2,1,0:T(8,128)(2,1)}), bf16[2,128,2048]{2,1,0:T(8,128)(2,1)}) %reduce-scatter.3.cloned.1.call-update) | async-done | bytes 1048592 | tf_op jit(solution)/shard_map/reduce_scatter | solution.py:110
  272.3 2.8 multiply_bitcast_fusion.1
  (79 shorter events, 18.7 us)
Async XLA Ops:
  7.2 5.7 %copy-start = (bf16[3,2,1,128,2048]{4,3,2,1,0:T(8,128)(2,1)S(1)}, bf16[3,2,1,128,2048]{4,3,2,1,0:T(8,128)(2,1)}, u32[]{:S(2)}) copy-start(bf16[3,2,1,128,2048]{4,3,2,1,0:T(8,128)(2,1)} %param.9) | copy-start | bytes 9437188
  7.2 31.7 %all-reduce.12.cloned.1.call-start = ((), (), s32[]{:S(2)}) async-start(), calls=%async_computation.6 | async-start | bytes 1048576 | tf_op jit(solution)/shard_map/psum | solution.py:28
  17.3 12.4 %copy-start.20 = (s32[2,1,4]{2,1,0:T(1,128)S(1)}, s32[2,1,4]{2,1,0:T(1,128)}, u32[]{:S(2)}) copy-start(s32[2,1,4]{2,1,0:T(1,128)} %param.16) | copy-start | bytes 100
  17.3 79.9 %all-reduce.10.cloned.1.call-start = ((), (), s32[]{:S(2)}) async-start(), calls=%async_computation.5 | async-start | bytes 1048576 | tf_op jit(solution)/shard_map/psum | solution.py:28
  45.3 26.8 %collective-permute-start = (bf16[2,128,2048]{2,1,0:T(8,128)(2,1)}, bf16[2,128,2048]{2,1,0:T(8,128)(2,1)}, u32[]{:S(2)}, u32[]{:S(2)}) collective-permute-start(bf16[2,128,2048]{2,1,0:T(8,128)(2,1)} %fusion.33), channel_id=1, source_target_pairs={{0,24},{8,0},{16,8},{24,16},{1,25},{9,1},{17,9},{25,17},{2,26},{10... | collective-permute-start | bytes 3145736 | tf_op jit(solution)/shard_map/ppermute | solution.py:14
  49.1 4.5 %copy-start.17 = (bf16[2,128,2048]{2,1,0:T(8,128)(2,1)S(1)}, bf16[2,128,2048]{2,1,0:T(8,128)(2,1)}, u32[]{:S(2)}) copy-start(bf16[2,128,2048]{2,1,0:T(8,128)(2,1)} %param.14) | copy-start | bytes 3145732
  53.6 20.7 %copy-start.1 = (bf16[2,1,512,2048]{3,2,1,0:T(8,128)(2,1)S(1)}, bf16[2,1,512,2048]{3,2,1,0:T(8,128)(2,1)}, u32[]{:S(2)}) copy-start(bf16[2,1,512,2048]{3,2,1,0:T(8,128)(2,1)} %param.11) | copy-start | bytes 12582916
  53.9 18.2 %copy-start.3 = (bf16[2,128,2048]{2,1,0:T(8,128)(2,1)}, bf16[2,128,2048]{2,1,0:T(8,128)(2,1)S(1)}, u32[]{:S(2)}) copy-start(bf16[2,128,2048]{2,1,0:T(8,128)(2,1)S(1)} %multiply_convert_fusion) | copy-start | bytes 3145732
  73.4 1.0 copy-start.13
  76.6 76.8 %all-reduce.8.cloned.1.call-start = ((), (), s32[]{:S(2)}) async-start(), calls=%async_computation.4 | async-start | bytes 1048576 | tf_op jit(solution)/shard_map/psum | solution.py:28
  98.7 7.8 %copy-start.21 = (bf16[2,1,512,2048]{3,2,1,0:T(8,128)(2,1)S(1)}, bf16[2,1,512,2048]{3,2,1,0:T(8,128)(2,1)}, u32[]{:S(2)}) copy-start(bf16[2,1,512,2048]{3,2,1,0:T(8,128)(2,1)} %param.10) | copy-start | bytes 12582916
  102.8 26.6 %copy-start.4 = (bf16[2,128,2048]{2,1,0:T(8,128)(2,1)S(1)}, bf16[2,128,2048]{2,1,0:T(8,128)(2,1)}, u32[]{:S(2)}) copy-start(bf16[2,128,2048]{2,1,0:T(8,128)(2,1)} %copy-done.3) | copy-start | bytes 3145732
  102.8 27.6 %copy-start.2 = (bf16[2,1,512,2048]{3,2,1,0:T(8,128)(2,1)S(1)}, bf16[2,1,512,2048]{3,2,1,0:T(8,128)(2,1)}, u32[]{:S(2)}) copy-start(bf16[2,1,512,2048]{3,2,1,0:T(8,128)(2,1)} %param.11) | copy-start | bytes 12582916
  102.8 26.5 %collective-permute-start.1 = (bf16[2,128,2048]{2,1,0:T(8,128)(2,1)S(1)}, bf16[2,128,2048]{2,1,0:T(8,128)(2,1)S(1)}, u32[]{:S(2)}, u32[]{:S(2)}) collective-permute-start(bf16[2,128,2048]{2,1,0:T(8,128)(2,1)S(1)} %fusion.39), channel_id=1, source_target_pairs={{0,24},{8,0},{16,8},{24,16},{1,25},{9,1},{17,9},{25,17},{2,26},{10... | collective-permute-start | bytes 3145736 | tf_op jit(solution)/shard_map/ppermute | solution.py:14
  129.5 3.4 %copy-start.6 = (bf16[2,128,512]{2,1,0:T(8,128)(2,1)S(1)}, bf16[2,128,512]{2,1,0:T(8,128)(2,1)}, u32[]{:S(2)}) copy-start(bf16[2,128,512]{2,1,0:T(8,128)(2,1)} %get-tuple-element.17) | copy-start | bytes 786436
  132.6 84.2 %reduce-scatter.5.cloned.1.call-start = ((), (), s32[]{:S(2)}) async-start(), calls=%async_computation.3 | async-start | bytes 5242880 | tf_op jit(solution)/shard_map/reduce_scatter | solution.py:113
  132.9 6.0 %copy-start.7 = (bf16[2,128,512]{2,1,0:T(8,128)(2,1)S(1)}, bf16[2,128,512]{2,1,0:T(8,128)(2,1)}, u32[]{:S(2)}) copy-start(bf16[2,128,512]{2,1,0:T(8,128)(2,1)} %get-tuple-element.15) | copy-start | bytes 786436
  132.9 6.0 %copy-start.12 = (bf16[1,128,2048]{2,1,0:T(8,128)(2,1)S(1)}, bf16[1,128,2048]{2,1,0:T(8,128)(2,1)}, u32[]{:S(2)}) copy-start(bf16[1,128,2048]{2,1,0:T(8,128)(2,1)} %copy-done.11) | copy-start | bytes 1572868
  132.9 5.9 %copy-start.14 = (bf16[1,128,2048]{2,1,0:T(8,128)(2,1)S(1)}, bf16[1,128,2048]{2,1,0:T(8,128)(2,1)}, u32[]{:S(2)}) copy-start(bf16[1,128,2048]{2,1,0:T(8,128)(2,1)} %copy-done.13) | copy-start | bytes 1572868
  162.9 109.4 %reduce-scatter.3.cloned.1.call-start = ((), (), s32[]{:S(2)}) async-start(), calls=%async_computation.2 | async-start | bytes 5242880 | tf_op jit(solution)/shard_map/reduce_scatter | solution.py:110
  162.9 2.5 copy-start.8
  162.9 2.5 copy-start.16
  165.4 1.5 copy-start.5
  165.4 1.5 copy-start.15
  (5 other events, 4.1 us)
Sparse Core Ops, SparseCore 0:
  17.4 21.3 all-reduce.11
  76.7 20.5 all-reduce.9
  132.8 20.5 all-reduce.7
  163.0 53.7 reduce-scatter.4
  219.6 52.6 reduce-scatter.2
where the time goes:
time: 282 us
  waiting for transfers between devices  169 us (60%)
  matrix products  61.7 us (22%)
  between operations  14.1 us (5%)
  blocking collectives  13.8 us (5%)
  other arithmetic  12.9 us (5%)
  starting transfers between devices  7.7 us (3%)
  local copies, waits for them, and re-layouts  2.86 us (1%)
    reduce_scatter x1, waiting for transfers between devices, shards(): lax.psum_scatter((acc_in + add_in).astype(jnp.bfloat16), 'dp', scatter_di...  52.7 us
    reduce_scatter x1, waiting for transfers between devices, shards(): lax.psum_scatter((acc_out + add_out).astype(jnp.bfloat16), 'dp', scatter_...  40 us
    ppermute x2, waiting for transfers between devices, shifted(): return lax.ppermute(x, axis, [(i, (i + by) % count) for i in range(count)])  38.8 us
    psum x3, waiting for transfers between devices, block_back(): lax.psum(part_pre.astype(jnp.bfloat16), 'tensor').astype(jnp.float32)  37 us
    dot_general x3, matrix products, block_back(): jnp.einsum('vrk,vrd->vkd', hidden, arrive, preferred_element_type=jnp.flo...  20 us
    dot_general x3, matrix products, block_back(): jnp.einsum('vrk,vkd->vrd', grad_scaled, weight_in, preferred_element_type...  13.9 us
    psum x1, blocking collectives, shards(): sums, counts = lax.psum((sums, counts), 'dp')  11.4 us
    dot_general x3, matrix products, block_back(): jnp.einsum('vrd,vkd->vrk', gained, weight_in, preferred_element_type=jnp....  11.1 us
  transfers between devices with their start and end apart: 7, of which 7 were waited for; matrix products, arithmetic and copies ran while one was open for 13% of the time, Pallas kernels for 0%

commit v1 on v0

v1 whole, which is shorter than its diff:
```python
import functools

import jax
import jax.numpy as jnp
from jax import lax
from jax.experimental import pallas as pl
from jax.experimental.pallas import tpu as pltpu
from jax.sharding import PartitionSpec as P

EPS = 1e-05
MESH = pl.DeviceIdType.MESH
F32 = jnp.float32
BF16 = jnp.bfloat16


def dot_nt(a, b):
    return lax.dot_general(a, b, (((1,), (1,)), ((), ())), preferred_element_type=F32)


def dot_tn(a, b):
    return lax.dot_general(a, b, (((0,), (0,)), ((), ())), preferred_element_type=F32)


def factors(n):
    low = 1
    for k in range(1, n + 1):
        if n % k == 0 and k * k <= n:
            low = k
    return low, n // low


def kernel(
    dims,
    x_hbm, wi_hbm, wo_hbm, gn_ref, ar_hbm, lp_hbm, st_ref, hot_ref,
    gi_hbm, go_hbm, lv_hbm,
    xs, gd, ca, wi, wo, lp, ps, pr, presum, slope, hid, gs, bs, br, ob, lv,
    sqs, sqr, inv_t, str_, gbi, gbo, r1i, r1o, p2i, p2o, r2i, r2o, fi, fo,
    in_sem, out_sem, sq_sem, st_sem, pre_sem, back_sem, pipe_s, pipe_r, r1_s, r1_r, r2_s, r2_r,
):
    steps, vs, tok, wid, rank, nt, npipe, ndp = dims
    na, nb = factors(ndp)
    rc = rank // ndp
    full = wid * nt
    tile = min(256, wid)
    rtile = min(256, rank)
    me_t = lax.axis_index("tensor")
    me_p = lax.axis_index("pipe")
    me_d = lax.axis_index("dp")
    me_h = me_d // nb
    me_l = me_d % nb
    prev_p = lax.rem(me_p + npipe - 1, npipe)
    next_p = lax.rem(me_p + 1, npipe)

    def load(src, dst, k):
        return pltpu.make_async_copy(src, dst, in_sem.at[k])

    loads = [
        load(x_hbm, xs, 0),
        load(wi_hbm.at[1], wi.at[1], 1),
        load(wi_hbm.at[0], wi.at[0], 2),
        load(ar_hbm.at[1], ca.at[1, 0], 3),
        load(wo_hbm.at[1], wo.at[1], 4),
        load(ar_hbm.at[0], ca.at[0, 0], 5),
        load(wo_hbm.at[0], wo.at[0], 6),
        load(lp_hbm, lp, 7),
    ]
    for item in loads:
        item.start()

    barrier = pltpu.get_barrier_semaphore()
    for k in range(1, nt):
        pl.semaphore_signal(barrier, inc=1, device_id={"tensor": lax.rem(me_t + k, nt)}, device_id_type=MESH)
    for k in range(1, ndp):
        pl.semaphore_signal(barrier, inc=1, device_id={"dp": lax.rem(me_d + k, ndp)}, device_id_type=MESH)
    for other in (prev_p, next_p):
        pl.semaphore_signal(barrier, inc=1, device_id={"pipe": other}, device_id_type=MESH)
    pl.semaphore_wait(barrier, nt - 1 + ndp - 1 + 2)

    def to_tensor(src, dst_of, send_of, recv_of):
        return [
            pltpu.make_async_remote_copy(
                src_ref=src, dst_ref=dst_of(k - 1), send_sem=send_of(k - 1), recv_sem=recv_of(k - 1),
                device_id={"tensor": lax.rem(me_t + k, nt)}, device_id_type=MESH,
            )
            for k in range(1, nt)
        ]

    def to_dp(src_of, dst_of, send_of, recv_of, kind):
        out = []
        count = {"all": ndp, "h": na, "l": nb}[kind]
        for k in range(1, count):
            if kind == "all":
                who = lax.rem(me_d + k, ndp)
                part = who
            elif kind == "h":
                part = lax.rem(me_h + k, na)
                who = part * nb + me_l
            else:
                part = lax.rem(me_l + k, nb)
                who = me_h * nb + part
            out.append(
                pltpu.make_async_remote_copy(
                    src_ref=src_of(part), dst_ref=dst_of(k - 1), send_sem=send_of(k - 1), recv_sem=recv_of(k - 1),
                    device_id={"dp": who}, device_id_type=MESH,
                )
            )
        return out

    stat_copies = to_dp(lambda part: st_ref, lambda k: str_.at[k], lambda k: st_sem.at[0, k], lambda k: st_sem.at[1, k], "all")
    for item in stat_copies:
        item.start()

    loads[0].wait()
    lane = lax.broadcasted_iota(jnp.int32, (tok, 128), 1)
    sqs[...] = jnp.zeros_like(sqs)

    def prep(i, carry):
        t = i // vs
        v = i % vs
        row = xs[t, v].astype(F32)
        gd[v, pl.ds(pl.multiple_of(t * tok, tok), tok), :] = (row * gn_ref[v]).astype(BF16)
        squares = jnp.sum(row * row, axis=-1, keepdims=True)
        sqs[...] = jnp.where(lane == i, squares, sqs[...])
        return carry

    lax.fori_loop(0, steps * vs, prep, 0)
    sq_copies = to_tensor(sqs, lambda k: sqr.at[k], lambda k: sq_sem.at[0, k], lambda k: sq_sem.at[1, k])
    for item in sq_copies:
        item.start()

    pre_copies = {}
    back_copies = {}

    def pre_part(v):
        def body(j, carry):
            cols = pl.ds(pl.multiple_of(j * rtile, rtile), rtile)
            ps[v, :, cols] = dot_nt(gd[v], wi[v, cols, :]).astype(BF16)
            return carry

        lax.fori_loop(0, rank // rtile, body, 0)
        pre_copies[v] = to_tensor(
            ps.at[v], lambda k: pr.at[k, v], lambda k: pre_sem.at[0, v, k], lambda k: pre_sem.at[1, v, k]
        )
        for item in pre_copies[v]:
            item.start()

    def back_part(t, v):
        def body(j, carry):
            cols = pl.ds(pl.multiple_of(j * rtile, rtile), rtile)
            bs[v, t, :, cols] = dot_nt(ca[v, t], wo[v, cols, :]).astype(BF16)
            return carry

        lax.fori_loop(0, rank // rtile, body, 0)
        back_copies[t, v] = to_tensor(
            bs.at[v, t], lambda k: br.at[k, v, t],
            lambda k: back_sem.at[0, v * steps + t, k], lambda k: back_sem.at[1, v * steps + t, k],
        )
        for item in back_copies[t, v]:
            item.start()

    def finish_pre(v):
        for item in pre_copies[v]:
            item.wait_recv()
        for t in range(steps):
            rows = pl.ds(t * tok, tok)
            total = ps[v, rows, :].astype(F32)
            for k in range(nt - 1):
                total = total + pr[k, v, rows, :].astype(F32)
            index = t * vs + v
            pre = inv_t[:, index:index + 1] * total
            sigma = jax.nn.sigmoid(pre)
            presum[v, rows, :] = total
            hid[v, rows, :] = (pre * sigma).astype(BF16)
            slope[v, rows, :] = sigma * (1.0 + pre * (1.0 - sigma))

    def finish_back(t, v):
        for item in back_copies[t, v]:
            item.wait_recv()
        rows = pl.ds(t * tok, tok)
        index = t * vs + v
        inv = inv_t[:, index:index + 1]
        total = bs[v, t].astype(F32)
        for k in range(nt - 1):
            total = total + br[k, v, t].astype(F32)
        grad_pre = total * slope[v, rows, :]
        gs[v, rows, :] = (inv * grad_pre).astype(BF16)
        radial = jnp.sum(grad_pre * presum[v, rows, :], axis=-1, keepdims=True)
        coef = inv * inv * inv * radial * (1.0 / full)

        def body(j, carry):
            cols = pl.ds(pl.multiple_of(j * tile, tile), tile)
            lifted = jnp.dot(gs[v, rows, :], wi[v, :, cols], preferred_element_type=F32)
            out = (
                ca[v, t, :, cols].astype(F32)
                + gn_ref[v, :, cols] * lifted
                - xs[t, v, :, cols].astype(F32) * coef
            ).astype(BF16)
            if t < steps - 1:
                ob[t, v, :, cols] = out
            else:
                lv[v, :, cols] = out
            return carry

        lax.fori_loop(0, wid // tile, body, 0)

    def pipe_copy(t, v, slot):
        return pltpu.make_async_remote_copy(
            src_ref=ob.at[t, v], dst_ref=ca.at[slot, t + 1],
            send_sem=pipe_s.at[t, v], recv_sem=pipe_r.at[t, slot],
            device_id={"pipe": prev_p}, device_id_type=MESH,
        )

    def send_on(t, v):
        @pl.when(me_p > 0)
        def _():
            pipe_copy(t, v, v).start()

        if v == 1:
            @pl.when(me_p == 0)
            def _():
                pipe_copy(t, 1, 0).start()

    def sent_on(t, v):
        @pl.when(me_p > 0)
        def _():
            pipe_copy(t, v, v).wait_send()

        if v == 1:
            @pl.when(me_p == 0)
            def _():
                pipe_copy(t, 1, 0).wait_send()

    def take(t, v):
        if v == 0:
            pipe_copy(t - 1, v, v).wait_recv()
        else:
            @pl.when(me_p < npipe - 1)
            def _():
                pipe_copy(t - 1, v, v).wait_recv()

            @pl.when(me_p == npipe - 1)
            def _():
                stats = st_ref[...]
                for k in range(ndp - 1):
                    stats = stats + str_[k]
                means = stats[0:1] / jnp.maximum(stats[1:2], 1.0) + stats[2:3] * (1.0 / ndp)
                weight = jnp.sum(hot_ref[t - 1] * means, axis=-1, keepdims=True)
                ca[1, t] = (weight * lp[t - 1].astype(F32)).astype(BF16)

    def grad_cols(left_ref, right_of, dest, v):
        def body(j, carry):
            cols = pl.ds(pl.multiple_of(j * tile, tile), tile)
            value = dot_tn(left_ref[v], right_of(v, cols)).astype(BF16)
            dest[v, :, :, :, cols] = value.reshape(na, nb, rc, tile)
            return carry

        lax.fori_loop(0, wid // tile, body, 0)

    def copies_one(which, v):
        base = which * vs + v
        if which == 0:
            return to_dp(
                lambda part: gbi.at[v, part], lambda k: r1i.at[v, k],
                lambda k: r1_s.at[base, k], lambda k: r1_r.at[base, k], "h",
            )
        return to_dp(
            lambda part: gbo.at[v, :, part], lambda k: r1o.at[v, k],
            lambda k: r1_s.at[base, k], lambda k: r1_r.at[base, k], "l",
        )

    def copies_two(which, v):
        base = which * vs + v
        if which == 0:
            return to_dp(
                lambda part: p2i.at[v, part], lambda k: r2i.at[v, k],
                lambda k: r2_s.at[base, k], lambda k: r2_r.at[base, k], "l",
            )
        return to_dp(
            lambda part: p2o.at[v, part], lambda k: r2o.at[v, k],
            lambda k: r2_s.at[base, k], lambda k: r2_r.at[base, k], "h",
        )

    def middle(which, v):
        for item in copies_one(which, v):
            item.wait_recv()
        if which == 0:
            total = gbi[v, me_h].astype(F32)
            for k in range(na - 1):
                total = total + r1i[v, k].astype(F32)
            p2i[v] = total.astype(BF16)
        else:
            total = gbo[v, :, me_l].astype(F32)
            for k in range(nb - 1):
                total = total + r1o[v, k].astype(F32)
            p2o[v] = total.astype(BF16)
        for item in copies_two(which, v):
            item.start()

    scale = 1.0 / (ndp * tok)

    def final(which, v):
        for item in copies_two(which, v):
            item.wait_recv()
        if which == 0:
            total = p2i[v, me_l].astype(F32)
            for k in range(nb - 1):
                total = total + r2i[v, k].astype(F32)
            fi[v] = total * scale
            copy = pltpu.make_async_copy(fi.at[v], gi_hbm.at[v], out_sem.at[v])
        else:
            total = p2o[v, me_h].astype(F32)
            for k in range(na - 1):
                total = total + r2o[v, k].astype(F32)
            fo[v] = total * scale
            copy = pltpu.make_async_copy(fo.at[v], go_hbm.at[v], out_sem.at[vs + v])
        copy.start()
        return copy

    loads[1].wait()
    pre_part(1)
    loads[3].wait()
    loads[4].wait()
    back_part(0, 1)
    for item in sq_copies:
        item.wait_recv()
    total_sq = sqs[...]
    for k in range(nt - 1):
        total_sq = total_sq + sqr[k]
    inv_t[...] = 1.0 / jnp.sqrt(total_sq * (1.0 / full) + EPS)
    loads[2].wait()
    pre_part(0)
    finish_pre(1)
    finish_back(0, 1)
    send_on(0, 1)
    loads[5].wait()
    loads[6].wait()
    back_part(0, 0)
    finish_pre(0)
    finish_back(0, 0)
    send_on(0, 0)
    loads[7].wait()
    for item in stat_copies:
        item.wait_recv()
    stored = []
    for t in range(1, steps):
        for v in (1, 0):
            take(t, v)
            back_part(t, v)
            if t == steps - 1:
                grad_cols(hid, lambda u, cols: ca[u, :, :, cols].reshape(steps * tok, tile), gbo, v)
                for item in copies_one(1, v):
                    item.start()
            finish_back(t, v)
            if t < steps - 1:
                send_on(t, v)
            else:
                grad_cols(gs, lambda u, cols: gd[u, :, cols], gbi, v)
                for item in copies_one(0, v):
                    item.start()
                copy = pltpu.make_async_copy(lv.at[v], lv_hbm.at[v], out_sem.at[2 * vs + v])
                copy.start()
                stored.append(copy)
    for v in (1, 0):
        middle(1, v)
        middle(0, v)
    for v in (1, 0):
        stored.append(final(1, v))
        stored.append(final(0, v))
    for item in stat_copies + sq_copies:
        item.wait_send()
    for v in range(vs):
        for item in pre_copies[v]:
            item.wait_send()
        for t in range(steps):
            for item in back_copies[t, v]:
                item.wait_send()
            if t < steps - 1:
                sent_on(t, v)
        for which in range(2):
            for item in copies_one(which, v) + copies_two(which, v):
                item.wait_send()
    for item in stored:
        item.wait()


def shards(
    saved_inputs, proj_in, proj_out, norm_gain, arriving, logp_grad, rewards, seq_lengths, group_ids
):
    nt = lax.axis_size("tensor")
    npipe = lax.axis_size("pipe")
    ndp = lax.axis_size("dp")
    steps, vs, _, tok, wid = saved_inputs.shape
    rank = proj_in.shape[2]
    new_count = logp_grad.shape[0]
    seq_count = rewards.shape[2]
    group_count = new_count * ndp * seq_count // 8
    lanes = -(-(group_count + 1) // 128) * 128
    na, nb = factors(ndp)
    rc = rank // ndp

    groups = jnp.arange(lanes, dtype=jnp.int32)
    member = (group_ids[..., None] == groups).astype(F32)
    sums = jnp.sum(member * rewards[..., None], axis=(0, 1, 2))
    counts = jnp.sum(member, axis=(0, 1, 2))
    unit = (groups == group_count).astype(F32)
    blank = jnp.zeros_like(unit)
    stats = jnp.stack([sums, counts, unit, blank, blank, blank, blank, blank])
    ends = jnp.cumsum(seq_lengths[:, 0], axis=-1)
    position = jnp.arange(tok, dtype=jnp.int32)
    starts = ends - seq_lengths[:, 0]
    pick = (position[:, None] >= starts[:, None, :]) & (position[:, None] < ends[:, None, :])
    seq_rows = member[:, 0] - unit * rewards[:, 0, :, None]
    hot = jnp.sum(jnp.where(pick[..., None], seq_rows[:, None], 0.0), axis=2)

    dims = (steps, vs, tok, wid, rank, nt, npipe, ndp)
    peers = max(nt - 1, 1)
    any_spec = pl.BlockSpec(memory_space=pl.ANY)
    vmem = pl.BlockSpec(memory_space=pltpu.VMEM)
    V = pltpu.VMEM
    DMA = pltpu.SemaphoreType.DMA
    pmax = max(na, nb)
    scratch = [
        V((steps, vs, tok, wid), BF16),
        V((vs, steps * tok, wid), BF16),
        V((vs, steps, tok, wid), BF16),
        V((vs, rank, wid), BF16),
        V((vs, rank, wid), BF16),
        V((new_count, tok, wid), BF16),
        V((vs, steps * tok, rank), BF16),
        V((peers, vs, steps * tok, rank), BF16),
        V((vs, steps * tok, rank), F32),
        V((vs, steps * tok, rank), F32),
        V((vs, steps * tok, rank), BF16),
        V((vs, steps * tok, rank), BF16),
        V((vs, steps, tok, rank), BF16),
        V((peers, vs, steps, tok, rank), BF16),
        V((steps - 1, vs, tok, wid), BF16),
        V((vs, tok, wid), BF16),
        V((tok, 128), F32),
        V((peers, tok, 128), F32),
        V((tok, 128), F32),
        V((max(ndp - 1, 1), 8, lanes), F32),
        V((vs, na, nb, rc, wid), BF16),
        V((vs, na, nb, rc, wid), BF16),
        V((vs, max(na - 1, 1), nb, rc, wid), BF16),
        V((vs, max(nb - 1, 1), na, rc, wid), BF16),
        V((vs, nb, rc, wid), BF16),
        V((vs, na, rc, wid), BF16),
        V((vs, max(nb - 1, 1), rc, wid), BF16),
        V((vs, max(na - 1, 1), rc, wid), BF16),
        V((vs, rc, wid), F32),
        V((vs, rc, wid), F32),
        DMA((8,)),
        DMA((3 * vs,)),
        DMA((2, peers)),
        DMA((2, max(ndp - 1, 1))),
        DMA((2, vs, peers)),
        DMA((2, vs * steps, peers)),
        DMA((steps - 1, vs)),
        DMA((steps - 1, vs)),
        DMA((2 * vs, pmax)),
        DMA((2 * vs, pmax)),
        DMA((2 * vs, pmax)),
        DMA((2 * vs, pmax)),
    ]
    grad_in, grad_out, leaving = pl.pallas_call(
        functools.partial(kernel, dims),
        out_shape=(
            jax.ShapeDtypeStruct((vs, rc, wid), F32),
            jax.ShapeDtypeStruct((vs, rc, wid), F32),
            jax.ShapeDtypeStruct((vs, tok, wid), BF16),
        ),
        in_specs=[any_spec, any_spec, any_spec, vmem, any_spec, any_spec, vmem, vmem],
        out_specs=(any_spec, any_spec, any_spec),
        scratch_shapes=scratch,
        compiler_params=pltpu.CompilerParams(
            collective_id=0, has_side_effects=True, vmem_limit_bytes=67043328
        ),
    )(
        saved_inputs[:, :, 0], proj_in[:, 0], proj_out[:, 0], norm_gain, arriving[:, 0], logp_grad, stats, hot
    )
    return grad_in[:, None], grad_out[:, None], leaving[:, None]


def solution(mesh):
    return jax.shard_map(
        shards,
        mesh=mesh,
        in_specs=(
            P(None, None, "pipe", "dp", "tensor"),
            P(None, "pipe", None, "tensor"),
            P(None, "pipe", None, "tensor"),
            P(None, "pipe", "tensor"),
            P(None, "pipe", "dp", "tensor"),
            P(None, "dp", "tensor"),
            P(None, "dp", None),
            P(None, "dp", None),
            P(None, "dp", None),
        ),
        out_specs=(
            P(None, "pipe", "dp", "tensor"),
            P(None, "pipe", "dp", "tensor"),
            P(None, "pipe", "dp", "tensor"),
        ),
        check_vma=False,
    )
```

time: 282 us -> 139 us (0.49)
  waiting for transfers between devices: 169 us -> 0 us
  Pallas kernels: 0 us -> 127 us
  matrix products: 61.7 us -> 0 us
  blocking collectives: 13.8 us -> 0 us
  between operations: 14.1 us -> 0.68 us
  other arithmetic: 12.9 us -> 4.03 us
  starting transfers between devices: 7.7 us -> 0 us
  local copies, waits for them, and re-layouts: 2.86 us -> 6.83 us
    pallas_call x0 -> x1, Pallas kernels: none -> 127 us  [shards(): pl.pallas_call(functools.partial(kernel, dims), out_shape=(jax.ShapeDtype...]
    reduce_scatter x2 -> x0, waiting for transfers between devices: 92.7 us -> none  [the longest x1 52.7 us: shards(): lax.psum_scatter((acc_in + add_in).astype(jnp.bfloat16), 'dp', scatter_di...]
    dot_general x15 -> x0, matrix products: 61.7 us -> none  [the longest x3 20 us: block_back(): jnp.einsum('vrk,vrd->vkd', hidden, arrive, preferred_element_type=jnp.flo...]
    ppermute x2 -> x0, waiting for transfers between devices: 38.8 us -> none  [shifted(): return lax.ppermute(x, axis, [(i, (i + by) % count) for i in range(count)])]
    psum x3 -> x0, waiting for transfers between devices: 37 us -> none  [block_back(): lax.psum(part_pre.astype(jnp.bfloat16), 'tensor').astype(jnp.float32)]
    psum x2 -> x0, blocking collectives: 13.8 us -> none  [the longest x1 11.4 us: shards(): sums, counts = lax.psum((sums, counts), 'dp')]
    ppermute x2 -> x0, starting transfers between devices: 7.31 us -> none  [shifted(): return lax.ppermute(x, axis, [(i, (i + by) % count) for i in range(count)])]
    unnamed x2 -> x0, other arithmetic: 5.57 us -> none
  transfers between devices with their start and end apart: 7 -> 0, of which waited for: 7 -> 0; matrix products, arithmetic and copies ran while one was open for 13% -> 0% of each run, Pallas kernels for 0% -> 0%
where the time goes in v1:
time: 139 us
  Pallas kernels  127 us (91%)
  local copies, waits for them, and re-layouts  6.83 us (5%)
  other arithmetic  4.03 us (3%)
    pallas_call x1, Pallas kernels, shards(): pl.pallas_call(functools.partial(kernel, dims), out_shape=(jax.ShapeDtype...  127 us
    unnamed x7, local copies, waits for them, and re-layouts  6.22 us

profile of v1, /device:TPU:0, one launch (start us, length us, event | category | flops | bytes accessed | tf_op | source)
XLA Modules:
  0.0 138.5 jit_solution(16930587291944335580)
XLA Ops:
  0.7 0.9 reduce_window_sum.13
  1.5 0.7 fusion.1
  2.2 0.1 fusion
  2.3 0.8 convert_reduce_fusion
  3.1 0.6 stack.16.st_ref
  3.7 0.8 multiply_subtract_fusion
  4.4 0.9 select_reduce_fusion.hot_ref
  5.3 127.0 %shard_map.112 = (f32[2,128,2048]{2,1,0:T(8,128)}, f32[2,128,2048]{2,1,0:T(8,128)}, bf16[2,128,2048]{2,1,0:T(8,128)(2,1)}) custom-call(bf16[3,2,128,2048]{3,2,1,0:T(8,128)(2,1)} %bitcast.27, bf16[2,512,2048]{2,1,0:T(8,128)(2,1)} %bitcast.25, bf16[2,512,2048]{2,1,0:T(8,128)(2,1)} %bitcast.26, f32[2,1,2048]{2,1,0:T(1,128)} %gn_ref.1, ...), custom_call_target="tpu_custom_call" | custom-call | tf_op jit(solution)/shard_map/pallas_call | solution.py:466
  132.3 0.0 copy-start
  132.3 3.3 %copy.23 = f32[2,1,128,2048]{3,2,1,0:T(8,128)} copy(f32[2,1,128,2048]{3,2,1,0:T(8,128)} %bitcast.29) | data formatting | bytes 4194304
  135.6 0.0 copy-done
  135.6 0.0 copy-start.1
  135.6 1.3 copy.24
  136.9 0.6 copy-done.1
  137.5 1.0 copy.25
  (4 shorter events, 0.0 us)
Async XLA Ops:
  132.3 3.3 %copy-start = (f32[2,128,2048]{2,1,0:T(8,128)S(1)}, f32[2,128,2048]{2,1,0:T(8,128)}, u32[]{:S(2)}) copy-start(f32[2,128,2048]{2,1,0:T(8,128)} %get-tuple-element.7) | copy-start | bytes 6291460
  135.6 2.0 %copy-start.1 = (bf16[2,128,2048]{2,1,0:T(8,128)(2,1)S(1)}, bf16[2,128,2048]{2,1,0:T(8,128)(2,1)}, u32[]{:S(2)}) copy-start(bf16[2,128,2048]{2,1,0:T(8,128)(2,1)} %get-tuple-element.8) | copy-start | bytes 3145732

commit v2 on v1

--- a/solution.py
+++ b/solution.py
@@ -17,10 +17,6 @@
     return lax.dot_general(a, b, (((1,), (1,)), ((), ())), preferred_element_type=F32)
 
 
-def dot_tn(a, b):
-    return lax.dot_general(a, b, (((0,), (0,)), ((), ())), preferred_element_type=F32)
-
-
 def factors(n):
     low = 1
     for k in range(1, n + 1):
@@ -31,11 +27,12 @@
 
 def kernel(
     dims,
-    x_hbm, wi_hbm, wo_hbm, gn_ref, ar_hbm, lp_hbm, st_ref, hot_ref,
-    gi_hbm, go_hbm, lv_hbm,
-    xs, gd, ca, wi, wo, lp, ps, pr, presum, slope, hid, gs, bs, br, ob, lv,
-    sqs, sqr, inv_t, str_, gbi, gbo, r1i, r1o, p2i, p2o, r2i, r2o, fi, fo,
-    in_sem, out_sem, sq_sem, st_sem, pre_sem, back_sem, pipe_s, pipe_r, r1_s, r1_r, r2_s, r2_r,
+    x_hbm, wi_hbm, wo_hbm, gn_ref, ar_hbm, lp_hbm, rew_ref, len_ref, ids_ref,
+    fi, fo, lv,
+    xs, gd, ca, wi, wo, lp, ps, pr, presum, slope, hid_t, gs, gs_t, gsr0, gsr1, gdr0, gdr1, bs, br, ob,
+    sqs, sqr, inv_t, stl, str_, gba, gbb, r1a, r1b, p2a, p2b, r2a, r2b, p2i0, p2i1, r2i0, r2i1,
+    in_sem, sq_sem, st_sem, pre_sem, back_sem, pipe_s, pipe_r, gd_s, gd_r, gt_s, gt_r,
+    r1_s, r1_r, r2_s, r2_r,
 ):
     steps, vs, tok, wid, rank, nt, npipe, ndp = dims
     na, nb = factors(ndp)
@@ -43,6 +40,10 @@
     full = wid * nt
     tile = min(256, wid)
     rtile = min(256, rank)
+    half = wid // 2
+    lanes = stl.shape[1]
+    new_count, _, seq_count = rew_ref.shape
+    unit_lane = new_count * ndp * seq_count // 8
     me_t = lax.axis_index("tensor")
     me_p = lax.axis_index("pipe")
     me_d = lax.axis_index("dp")
@@ -66,6 +67,15 @@
     ]
     for item in loads:
         item.start()
+
+    lane8 = lax.broadcasted_iota(jnp.int32, (8, lanes), 1)
+    row8 = lax.broadcasted_iota(jnp.int32, (8, lanes), 0)
+    stats_own = jnp.where((row8 == 2) & (lane8 == unit_lane), 1.0, 0.0)
+    for n in range(new_count):
+        for k in range(seq_count):
+            value = jnp.where(row8 == 0, rew_ref[n, 0, k], jnp.where(row8 == 1, 1.0, 0.0))
+            stats_own = stats_own + jnp.where(lane8 == ids_ref[n, 0, k], value, 0.0)
+    stl[...] = stats_own
 
     barrier = pltpu.get_barrier_semaphore()
     for k in range(1, nt):
@@ -106,7 +116,7 @@
             )
         return out
 
-    stat_copies = to_dp(lambda part: st_ref, lambda k: str_.at[k], lambda k: st_sem.at[0, k], lambda k: st_sem.at[1, k], "all")
+    stat_copies = to_dp(lambda part: stl, lambda k: str_.at[k], lambda k: st_sem.at[0, k], lambda k: st_sem.at[1, k], "all")
     for item in stat_copies:
         item.start()
 
@@ -127,6 +137,29 @@
     sq_copies = to_tensor(sqs, lambda k: sqr.at[k], lambda k: sq_sem.at[0, k], lambda k: sq_sem.at[1, k])
     for item in sq_copies:
         item.start()
+
+    gather_kind = ("h", "l")
+    gdr = (gdr0, gdr1)
+    gsr = (gsr0, gsr1)
+
+    def gd_copies(v):
+        return to_dp(
+            lambda part: gd.at[v], lambda k: gdr[v].at[k],
+            lambda k: gd_s.at[v, k], lambda k: gd_r.at[v, k], gather_kind[v],
+        )
+
+    def gs_copies(t, v):
+        cols = pl.ds(t * tok, tok)
+        base = v * steps + t
+        source = (lambda part: gs_t.at[v, part, :, :, cols]) if v == 0 else (lambda part: gs_t.at[v, :, part, :, cols])
+        return to_dp(
+            source, lambda k: gsr[v].at[k, :, :, cols],
+            lambda k: gt_s.at[base, k], lambda k: gt_r.at[base, k], gather_kind[v],
+        )
+
+    for v in (1, 0):
+        for item in gd_copies(v):
+            item.start()
 
     pre_copies = {}
     back_copies = {}
@@ -170,7 +203,7 @@
             pre = inv_t[:, index:index + 1] * total
             sigma = jax.nn.sigmoid(pre)
             presum[v, rows, :] = total
-            hid[v, rows, :] = (pre * sigma).astype(BF16)
+            hid_t[v, :, rows] = jnp.transpose(pre * sigma).astype(BF16)
             slope[v, rows, :] = sigma * (1.0 + pre * (1.0 - sigma))
 
     def finish_back(t, v):
@@ -183,7 +216,14 @@
         for k in range(nt - 1):
             total = total + br[k, v, t].astype(F32)
         grad_pre = total * slope[v, rows, :]
-        gs[v, rows, :] = (inv * grad_pre).astype(BF16)
+        scaled = inv * grad_pre
+        gs[v, rows, :] = scaled.astype(BF16)
+        gs_t[v, :, :, :, rows] = jnp.transpose(scaled).astype(BF16).reshape(na, nb, rc, tok)
+        for item in gs_copies(t, v):
+            item.start()
+        if t == steps - 1:
+            for item in copies_one(0, v) + copies_one(1, v):
+                item.start()
         radial = jnp.sum(grad_pre * presum[v, rows, :], axis=-1, keepdims=True)
         coef = inv * inv * inv * radial * (1.0 / full)
 
@@ -240,59 +280,100 @@
 
             @pl.when(me_p == npipe - 1)
             def _():
-                stats = st_ref[...]
+                stats = stl[...]
                 for k in range(ndp - 1):
                     stats = stats + str_[k]
                 means = stats[0:1] / jnp.maximum(stats[1:2], 1.0) + stats[2:3] * (1.0 / ndp)
-                weight = jnp.sum(hot_ref[t - 1] * means, axis=-1, keepdims=True)
+                tok_row = lax.broadcasted_iota(jnp.int32, (tok, lanes), 0)
+                tok_lane = lax.broadcasted_iota(jnp.int32, (tok, lanes), 1)
+                hot = jnp.zeros((tok, lanes), F32)
+                begin = 0
+                for k in range(seq_count):
+                    finish = begin + len_ref[t - 1, 0, k]
+                    inside = (tok_row >= begin) & (tok_row < finish)
+                    value = jnp.where(tok_lane == ids_ref[t - 1, 0, k], 1.0, 0.0)
+                    value = value - jnp.where(tok_lane == unit_lane, rew_ref[t - 1, 0, k], 0.0)
+                    hot = hot + jnp.where(inside, value, 0.0)
+                    begin = finish
+                weight = jnp.sum(hot * means, axis=-1, keepdims=True)
                 ca[1, t] = (weight * lp[t - 1].astype(F32)).astype(BF16)
 
-    def grad_cols(left_ref, right_of, dest, v):
+    def grad_out(v):
+        def body(j, carry):
+            for dest, off in ((gba, 0), (gbb, half)):
+                cols = pl.ds(pl.multiple_of(j * tile, tile), tile)
+                from_cols = pl.ds(pl.multiple_of(off + j * tile, tile), tile)
+                right = ca[v, :, :, from_cols].reshape(steps * tok, tile)
+                value = jnp.dot(hid_t[v], right, preferred_element_type=F32).astype(BF16)
+                dest[v, :, :, :, cols] = value.reshape(na, nb, rc, tile)
+            return carry
+
+        lax.fori_loop(0, half // tile, body, 0)
+
+    def grad_in(v):
+        for item in gd_copies(v):
+            item.wait_recv()
+        for t in range(steps):
+            for item in gs_copies(t, v):
+                item.wait_recv()
+        own = gs_t[v, me_h] if v == 0 else gs_t[v, :, me_l]
+        width = nb if v == 0 else na
+        own = own.reshape(width * rc, steps * tok)
+        dest = p2i0 if v == 0 else p2i1
+
         def body(j, carry):
             cols = pl.ds(pl.multiple_of(j * tile, tile), tile)
-            value = dot_tn(left_ref[v], right_of(v, cols)).astype(BF16)
-            dest[v, :, :, :, cols] = value.reshape(na, nb, rc, tile)
+            value = jnp.dot(own, gd[v, :, cols], preferred_element_type=F32)
+            for k in range((na if v == 0 else nb) - 1):
+                left = gsr[v][k].reshape(width * rc, steps * tok)
+                value = value + jnp.dot(left, gdr[v][k, :, cols], preferred_element_type=F32)
+            dest[:, :, cols] = value.astype(BF16).reshape(width, rc, tile)
             return carry
 
         lax.fori_loop(0, wid // tile, body, 0)
+        for item in copies_two(2, v):
+            item.start()
 
     def copies_one(which, v):
         base = which * vs + v
         if which == 0:
             return to_dp(
-                lambda part: gbi.at[v, part], lambda k: r1i.at[v, k],
-                lambda k: r1_s.at[base, k], lambda k: r1_r.at[base, k], "h",
+                lambda part: gba.at[v, :, part], lambda k: r1a.at[v, k],
+                lambda k: r1_s.at[base, k], lambda k: r1_r.at[base, k], "l",
             )
         return to_dp(
-            lambda part: gbo.at[v, :, part], lambda k: r1o.at[v, k],
-            lambda k: r1_s.at[base, k], lambda k: r1_r.at[base, k], "l",
+            lambda part: gbb.at[v, part], lambda k: r1b.at[v, k],
+            lambda k: r1_s.at[base, k], lambda k: r1_r.at[base, k], "h",
         )
 
     def copies_two(which, v):
         base = which * vs + v
         if which == 0:
-            return to_dp(
-                lambda part: p2i.at[v, part], lambda k: r2i.at[v, k],
-                lambda k: r2_s.at[base, k], lambda k: r2_r.at[base, k], "l",
-            )
+            source, dest, kind = p2a.at[v], r2a.at[v], "h"
+        elif which == 1:
+            source, dest, kind = p2b.at[v], r2b.at[v], "l"
+        elif v == 1:
+            source, dest, kind = p2i1, r2i1, "h"
+        else:
+            source, dest, kind = p2i0, r2i0, "l"
         return to_dp(
-            lambda part: p2o.at[v, part], lambda k: r2o.at[v, k],
-            lambda k: r2_s.at[base, k], lambda k: r2_r.at[base, k], "h",
+            lambda part: source.at[part], lambda k: dest.at[k],
+            lambda k: r2_s.at[base, k], lambda k: r2_r.at[base, k], kind,
         )
 
     def middle(which, v):
         for item in copies_one(which, v):
             item.wait_recv()
         if which == 0:
-            total = gbi[v, me_h].astype(F32)
+            total = gba[v, :, me_l].astype(F32)
+            for k in range(nb - 1):
+                total = total + r1a[v, k].astype(F32)
+            p2a[v] = total.astype(BF16)
+        else:
+            total = gbb[v, me_h].astype(F32)
             for k in range(na - 1):
-                total = total + r1i[v, k].astype(F32)
-            p2i[v] = total.astype(BF16)
-        else:
-            total = gbo[v, :, me_l].astype(F32)
-            for k in range(nb - 1):
-                total = total + r1o[v, k].astype(F32)
-            p2o[v] = total.astype(BF16)
+                total = total + r1b[v, k].astype(F32)
+            p2b[v] = total.astype(BF16)
         for item in copies_two(which, v):
             item.start()
 
@@ -301,20 +382,16 @@
     def final(which, v):
         for item in copies_two(which, v):
             item.wait_recv()
-        if which == 0:
-            total = p2i[v, me_l].astype(F32)
-            for k in range(nb - 1):
-                total = total + r2i[v, k].astype(F32)
+        along_h = which == 0 or (which == 2 and v == 1)
+        source = {0: p2a.at[v], 1: p2b.at[v], 2: p2i1 if v == 1 else p2i0}[which]
+        got = {0: r2a.at[v], 1: r2b.at[v], 2: r2i1 if v == 1 else r2i0}[which]
+        total = source[me_h if along_h else me_l].astype(F32)
+        for k in range((na if along_h else nb) - 1):
+            total = total + got[k].astype(F32)
+        if which == 2:
             fi[v] = total * scale
-            copy = pltpu.make_async_copy(fi.at[v], gi_hbm.at[v], out_sem.at[v])
         else:
-            total = p2o[v, me_h].astype(F32)
-            for k in range(na - 1):
-                total = total + r2o[v, k].astype(F32)
-            fo[v] = total * scale
-            copy = pltpu.make_async_copy(fo.at[v], go_hbm.at[v], out_sem.at[vs + v])
-        copy.start()
-        return copy
+            fo[v, :, pl.ds(which * half, half)] = total * scale
 
     loads[1].wait()
     pre_part(1)
@@ -341,46 +418,40 @@
     loads[7].wait()
     for item in stat_copies:
         item.wait_recv()
-    stored = []
     for t in range(1, steps):
         for v in (1, 0):
             take(t, v)
             back_part(t, v)
             if t == steps - 1:
-                grad_cols(hid, lambda u, cols: ca[u, :, :, cols].reshape(steps * tok, tile), gbo, v)
-                for item in copies_one(1, v):
-                    item.start()
+                grad_out(v)
             finish_back(t, v)
             if t < steps - 1:
                 send_on(t, v)
-            else:
-                grad_cols(gs, lambda u, cols: gd[u, :, cols], gbi, v)
-                for item in copies_one(0, v):
-                    item.start()
-                copy = pltpu.make_async_copy(lv.at[v], lv_hbm.at[v], out_sem.at[2 * vs + v])
-                copy.start()
-                stored.append(copy)
+            elif v == 1:
+                grad_in(1)
+    middle(0, 1)
+    middle(1, 1)
+    grad_in(0)
+    middle(0, 0)
+    middle(1, 0)
     for v in (1, 0):
-        middle(1, v)
-        middle(0, v)
-    for v in (1, 0):
-        stored.append(final(1, v))
-        stored.append(final(0, v))
+        for which in (2, 0, 1):
+            final(which, v)
     for item in stat_copies + sq_copies:
         item.wait_send()
     for v in range(vs):
-        for item in pre_copies[v]:
+        for item in pre_copies[v] + gd_copies(v):
             item.wait_send()
         for t in range(steps):
-            for item in back_copies[t, v]:
+            for item in back_copies[t, v] + gs_copies(t, v):
                 item.wait_send()
             if t < steps - 1:
                 sent_on(t, v)
-        for which in range(2):
-            for item in copies_one(which, v) + copies_two(which, v):
+        for item in copies_one(0, v) + copies_one(1, v):
+            item.wait_send()
+        for which in range(3):
+            for item in copies_two(which, v):
                 item.wait_send()
-    for item in stored:
-        item.wait()
 
 
 def shards(
@@ -392,26 +463,12 @@
     steps, vs, _, tok, wid = saved_inputs.shape
     rank = proj_in.shape[2]
     new_count = logp_grad.shape[0]
-    seq_count = rewards.shape[2]
-    group_count = new_count * ndp * seq_count // 8
+    group_count = new_count * ndp * rewards.shape[2] // 8
     lanes = -(-(group_count + 1) // 128) * 128
     na, nb = factors(ndp)
     rc = rank // ndp
-
-    groups = jnp.arange(lanes, dtype=jnp.int32)
-    member = (group_ids[..., None] == groups).astype(F32)
-    sums = jnp.sum(member * rewards[..., None], axis=(0, 1, 2))
-    counts = jnp.sum(member, axis=(0, 1, 2))
-    unit = (groups == group_count).astype(F32)
-    blank = jnp.zeros_like(unit)
-    stats = jnp.stack([sums, counts, unit, blank, blank, blank, blank, blank])
-    ends = jnp.cumsum(seq_lengths[:, 0], axis=-1)
-    position = jnp.arange(tok, dtype=jnp.int32)
-    starts = ends - seq_lengths[:, 0]
-    pick = (position[:, None] >= starts[:, None, :]) & (position[:, None] < ends[:, None, :])
-    seq_rows = member[:, 0] - unit * rewards[:, 0, :, None]
-    hot = jnp.sum(jnp.where(pick[..., None], seq_rows[:, None], 0.0), axis=2)
-
+    half = wid // 2
+    hm, lm = max(na - 1, 1), max(nb - 1, 1)
     dims = (steps, vs, tok, wid, rank, nt, npipe, ndp)
     peers = max(nt - 1, 1)
     any_spec = pl.BlockSpec(memory_space=pl.ANY)
@@ -419,6 +476,7 @@
     V = pltpu.VMEM
     DMA = pltpu.SemaphoreType.DMA
     pmax = max(na, nb)
+    smem = pl.BlockSpec(memory_space=pltpu.SMEM)
     scratch = [
         V((steps, vs, tok, wid), BF16),
         V((vs, steps * tok, wid), BF16),
@@ -430,54 +488,65 @@
         V((peers, vs, steps * tok, rank), BF16),
         V((vs, steps * tok, rank), F32),
         V((vs, steps * tok, rank), F32),
+        V((vs, rank, steps * tok), BF16),
         V((vs, steps * tok, rank), BF16),
-        V((vs, steps * tok, rank), BF16),
+        V((vs, na, nb, rc, steps * tok), BF16),
+        V((hm, nb, rc, steps * tok), BF16),
+        V((lm, na, rc, steps * tok), BF16),
+        V((hm, steps * tok, wid), BF16),
+        V((lm, steps * tok, wid), BF16),
         V((vs, steps, tok, rank), BF16),
         V((peers, vs, steps, tok, rank), BF16),
         V((steps - 1, vs, tok, wid), BF16),
-        V((vs, tok, wid), BF16),
         V((tok, 128), F32),
         V((peers, tok, 128), F32),
         V((tok, 128), F32),
+        V((8, lanes), F32),
         V((max(ndp - 1, 1), 8, lanes), F32),
-        V((vs, na, nb, rc, wid), BF16),
-        V((vs, na, nb, rc, wid), BF16),
-        V((vs, max(na - 1, 1), nb, rc, wid), BF16),
-        V((vs, max(nb - 1, 1), na, rc, wid), BF16),
-        V((vs, nb, rc, wid), BF16),
-        V((vs, na, rc, wid), BF16),
-        V((vs, max(nb - 1, 1), rc, wid), BF16),
-        V((vs, max(na - 1, 1), rc, wid), BF16),
-        V((vs, rc, wid), F32),
-        V((vs, rc, wid), F32),
+        V((vs, na, nb, rc, half), BF16),
+        V((vs, na, nb, rc, half), BF16),
+        V((vs, lm, na, rc, half), BF16),
+        V((vs, hm, nb, rc, half), BF16),
+        V((vs, na, rc, half), BF16),
+        V((vs, nb, rc, half), BF16),
+        V((vs, hm, rc, half), BF16),
+        V((vs, lm, rc, half), BF16),
+        V((nb, rc, wid), BF16),
+        V((na, rc, wid), BF16),
+        V((lm, rc, wid), BF16),
+        V((hm, rc, wid), BF16),
         DMA((8,)),
-        DMA((3 * vs,)),
         DMA((2, peers)),
         DMA((2, max(ndp - 1, 1))),
         DMA((2, vs, peers)),
         DMA((2, vs * steps, peers)),
         DMA((steps - 1, vs)),
         DMA((steps - 1, vs)),
+        DMA((vs, pmax)),
+        DMA((vs, pmax)),
+        DMA((vs * steps, pmax)),
+        DMA((vs * steps, pmax)),
         DMA((2 * vs, pmax)),
         DMA((2 * vs, pmax)),
-        DMA((2 * vs, pmax)),
-        DMA((2 * vs, pmax)),
+        DMA((3 * vs, pmax)),
+        DMA((3 * vs, pmax)),
     ]
     grad_in, grad_out, leaving = pl.pallas_call(
         functools.partial(kernel, dims),
         out_shape=(
-            jax.ShapeDtypeStruct((vs, rc, wid), F32),
-            jax.ShapeDtypeStruct((vs, rc, wid), F32),
-            jax.ShapeDtypeStruct((vs, tok, wid), BF16),
+            V((vs, rc, wid), F32),
+            V((vs, rc, wid), F32),
+            V((vs, tok, wid), BF16),
         ),
-        in_specs=[any_spec, any_spec, any_spec, vmem, any_spec, any_spec, vmem, vmem],
-        out_specs=(any_spec, any_spec, any_spec),
+        in_specs=[any_spec, any_spec, any_spec, vmem, any_spec, any_spec, smem, smem, smem],
+        out_specs=(vmem, vmem, vmem),
         scratch_shapes=scratch,
         compiler_params=pltpu.CompilerParams(
-            collective_id=0, has_side_effects=True, vmem_limit_bytes=67043328
+            collective_id=0, has_side_effects=True, vmem_limit_bytes=56 * 1024 * 1024
         ),
     )(
-        saved_inputs[:, :, 0], proj_in[:, 0], proj_out[:, 0], norm_gain, arriving[:, 0], logp_grad, stats, hot
+        saved_inputs[:, :, 0], proj_in[:, 0], proj_out[:, 0], norm_gain, arriving[:, 0], logp_grad,
+        rewards, seq_lengths, group_ids,
     )
     return grad_in[:, None], grad_out[:, None], leaving[:, None]
 

time: 139 us -> 105 us (0.76)
  Pallas kernels: 127 us -> 101 us
  other arithmetic: 4.03 us -> 0 us
  local copies, waits for them, and re-layouts: 6.83 us -> 3.61 us
    pallas_call x1, Pallas kernels: 127 us -> 101 us  [shards(): pl.pallas_call(functools.partial(kernel, dims), out_shape=(V((vs, rc, wid...]
    unnamed x7 -> x3, local copies, waits for them, and re-layouts: 6.22 us -> 3.61 us
    reduce_sum x2 -> x0, other arithmetic: 1.65 us -> none  [the longest x1 0.86 us: shards(): hot = jnp.sum(jnp.where(pick[..., None], seq_rows[:, None], 0.0), axis=2)]
where the time goes in v2:
time: 105 us
  Pallas kernels  101 us (96%)
  local copies, waits for them, and re-layouts  3.61 us (3%)
    pallas_call x1, Pallas kernels, shards(): pl.pallas_call(functools.partial(kernel, dims), out_shape=(V((vs, rc, wid...  101 us
    unnamed x3, local copies, waits for them, and re-layouts  3.61 us

profile of v2, /device:TPU:0, one launch (start us, length us, event | category | flops | bytes accessed | tf_op | source)
XLA Modules:
  0.0 105.0 jit_solution(11107538355151552361)
XLA Ops:
  0.6 100.7 %shard_map.112 = (f32[2,128,2048]{2,1,0:T(8,128)S(1)}, f32[2,128,2048]{2,1,0:T(8,128)S(1)}, bf16[2,128,2048]{2,1,0:T(8,128)(2,1)S(1)}) custom-call(bf16[3,2,128,2048]{3,2,1,0:T(8,128)(2,1)} %bitcast.18, bf16[2,512,2048]{2,1,0:T(8,128)(2,1)} %bitcast.16, bf16[2,512,2048]{2,1,0:T(8,128)(2,1)} %bitcast.17, f32[2,1,2048]{2,1,0:T(1,128)} %gn_ref.1, ...), custom_call_target="tpu_custom_call" | custom-call | tf_op jit(solution)/shard_map/pallas_call | solution.py:534
  101.4 1.3 %copy.18 = f32[2,1,128,2048]{3,2,1,0:T(8,128)} copy(f32[2,1,128,2048]{3,2,1,0:T(8,128)S(1)} %bitcast.14) | data formatting | bytes 4194304
  102.7 1.3 %copy.19 = f32[2,1,128,2048]{3,2,1,0:T(8,128)} copy(f32[2,1,128,2048]{3,2,1,0:T(8,128)S(1)} %bitcast.13) | data formatting | bytes 4194304
  104.0 1.0 copy.20

commit v3 on v2

--- a/solution.py
+++ b/solution.py
@@ -56,14 +56,15 @@
         return pltpu.make_async_copy(src, dst, in_sem.at[k])
 
     loads = [
-        load(x_hbm, xs, 0),
-        load(wi_hbm.at[1], wi.at[1], 1),
-        load(wi_hbm.at[0], wi.at[0], 2),
-        load(ar_hbm.at[1], ca.at[1, 0], 3),
-        load(wo_hbm.at[1], wo.at[1], 4),
+        load(ar_hbm.at[1], ca.at[1, 0], 0),
+        load(wo_hbm.at[1], wo.at[1], 1),
+        load(x_hbm.at[:, 1], xs.at[:, 1], 2),
+        load(wi_hbm.at[1], wi.at[1], 3),
+        load(x_hbm.at[:, 0], xs.at[:, 0], 4),
         load(ar_hbm.at[0], ca.at[0, 0], 5),
         load(wo_hbm.at[0], wo.at[0], 6),
-        load(lp_hbm, lp, 7),
+        load(wi_hbm.at[0], wi.at[0], 7),
+        load(lp_hbm, lp, 8),
     ]
     for item in loads:
         item.start()
@@ -120,23 +121,31 @@
     for item in stat_copies:
         item.start()
 
-    loads[0].wait()
     lane = lax.broadcasted_iota(jnp.int32, (tok, 128), 1)
-    sqs[...] = jnp.zeros_like(sqs)
-
-    def prep(i, carry):
-        t = i // vs
-        v = i % vs
-        row = xs[t, v].astype(F32)
-        gd[v, pl.ds(pl.multiple_of(t * tok, tok), tok), :] = (row * gn_ref[v]).astype(BF16)
-        squares = jnp.sum(row * row, axis=-1, keepdims=True)
-        sqs[...] = jnp.where(lane == i, squares, sqs[...])
-        return carry
-
-    lax.fori_loop(0, steps * vs, prep, 0)
-    sq_copies = to_tensor(sqs, lambda k: sqr.at[k], lambda k: sq_sem.at[0, k], lambda k: sq_sem.at[1, k])
-    for item in sq_copies:
-        item.start()
+
+    def sq_copies(v):
+        return to_tensor(
+            sqs.at[v], lambda k: sqr.at[k, v], lambda k: sq_sem.at[0, v, k], lambda k: sq_sem.at[1, v, k]
+        )
+
+    def prep(v):
+        def body(t, squares_all):
+            row = xs[t, v].astype(F32)
+            gd[v, pl.ds(pl.multiple_of(t * tok, tok), tok), :] = (row * gn_ref[v]).astype(BF16)
+            squares = jnp.sum(row * row, axis=-1, keepdims=True)
+            return jnp.where(lane == t, squares, squares_all)
+
+        sqs[v] = lax.fori_loop(0, steps, body, jnp.zeros((tok, 128), F32))
+        for item in sq_copies(v) + gd_copies(v):
+            item.start()
+
+    def finish_sq(v):
+        for item in sq_copies(v):
+            item.wait_recv()
+        total = sqs[v]
+        for k in range(nt - 1):
+            total = total + sqr[k, v]
+        inv_t[v] = 1.0 / jnp.sqrt(total * (1.0 / full) + EPS)
 
     gather_kind = ("h", "l")
     gdr = (gdr0, gdr1)
@@ -157,10 +166,6 @@
             lambda k: gt_s.at[base, k], lambda k: gt_r.at[base, k], gather_kind[v],
         )
 
-    for v in (1, 0):
-        for item in gd_copies(v):
-            item.start()
-
     pre_copies = {}
     back_copies = {}
 
@@ -191,16 +196,13 @@
         for item in back_copies[t, v]:
             item.start()
 
-    def finish_pre(v):
-        for item in pre_copies[v]:
-            item.wait_recv()
-        for t in range(steps):
+    def finish_pre(v, which_steps):
+        for t in which_steps:
             rows = pl.ds(t * tok, tok)
             total = ps[v, rows, :].astype(F32)
             for k in range(nt - 1):
                 total = total + pr[k, v, rows, :].astype(F32)
-            index = t * vs + v
-            pre = inv_t[:, index:index + 1] * total
+            pre = inv_t[v, :, t:t + 1] * total
             sigma = jax.nn.sigmoid(pre)
             presum[v, rows, :] = total
             hid_t[v, :, rows] = jnp.transpose(pre * sigma).astype(BF16)
@@ -210,8 +212,7 @@
         for item in back_copies[t, v]:
             item.wait_recv()
         rows = pl.ds(t * tok, tok)
-        index = t * vs + v
-        inv = inv_t[:, index:index + 1]
+        inv = inv_t[v, :, t:t + 1]
         total = bs[v, t].astype(F32)
         for k in range(nt - 1):
             total = total + br[k, v, t].astype(F32)
@@ -243,40 +244,52 @@
 
         lax.fori_loop(0, wid // tile, body, 0)
 
-    def pipe_copy(t, v, slot):
-        return pltpu.make_async_remote_copy(
-            src_ref=ob.at[t, v], dst_ref=ca.at[slot, t + 1],
-            send_sem=pipe_s.at[t, v], recv_sem=pipe_r.at[t, slot],
-            device_id={"pipe": prev_p}, device_id_type=MESH,
-        )
-
-    def send_on(t, v):
+    half_tok = tok // 2
+
+    def pipe_copies(t, v, slot):
+        parts = [(0, half_tok), (half_tok, half_tok)] if slot == 0 else [(0, tok)]
+        return [
+            pltpu.make_async_remote_copy(
+                src_ref=ob.at[t, v, pl.ds(start, size)], dst_ref=ca.at[slot, t + 1, pl.ds(start, size)],
+                send_sem=pipe_s.at[t, v, k], recv_sem=pipe_r.at[t, slot, k],
+                device_id={"pipe": prev_p}, device_id_type=MESH,
+            )
+            for k, (start, size) in enumerate(parts)
+        ]
+
+    def send_on(t, v, first, last):
         @pl.when(me_p > 0)
         def _():
-            pipe_copy(t, v, v).start()
+            for item in pipe_copies(t, v, v)[first:last]:
+                item.start()
 
         if v == 1:
             @pl.when(me_p == 0)
             def _():
-                pipe_copy(t, 1, 0).start()
+                for item in pipe_copies(t, 1, 0):
+                    item.start()
 
     def sent_on(t, v):
         @pl.when(me_p > 0)
         def _():
-            pipe_copy(t, v, v).wait_send()
+            for item in pipe_copies(t, v, v):
+                item.wait_send()
 
         if v == 1:
             @pl.when(me_p == 0)
             def _():
-                pipe_copy(t, 1, 0).wait_send()
+                for item in pipe_copies(t, 1, 0):
+                    item.wait_send()
 
     def take(t, v):
         if v == 0:
-            pipe_copy(t - 1, v, v).wait_recv()
+            for item in pipe_copies(t - 1, v, v):
+                item.wait_recv()
         else:
             @pl.when(me_p < npipe - 1)
             def _():
-                pipe_copy(t - 1, v, v).wait_recv()
+                for item in pipe_copies(t - 1, v, v):
+                    item.wait_recv()
 
             @pl.when(me_p == npipe - 1)
             def _():
@@ -393,29 +406,35 @@
         else:
             fo[v, :, pl.ds(which * half, half)] = total * scale
 
+    loads[0].wait()
     loads[1].wait()
+    back_part(0, 1)
+    loads[2].wait()
+    prep(1)
+    loads[3].wait()
     pre_part(1)
-    loads[3].wait()
     loads[4].wait()
-    back_part(0, 1)
-    for item in sq_copies:
+    prep(0)
+    finish_sq(1)
+    for item in pre_copies[1]:
         item.wait_recv()
-    total_sq = sqs[...]
-    for k in range(nt - 1):
-        total_sq = total_sq + sqr[k]
-    inv_t[...] = 1.0 / jnp.sqrt(total_sq * (1.0 / full) + EPS)
-    loads[2].wait()
-    pre_part(0)
-    finish_pre(1)
+    finish_pre(1, [0])
     finish_back(0, 1)
-    send_on(0, 1)
+    send_on(0, 1, 0, 1)
     loads[5].wait()
     loads[6].wait()
     back_part(0, 0)
-    finish_pre(0)
+    loads[7].wait()
+    pre_part(0)
+    finish_pre(1, range(1, steps))
+    finish_sq(0)
+    for item in pre_copies[0]:
+        item.wait_recv()
+    finish_pre(0, [0])
     finish_back(0, 0)
-    send_on(0, 0)
-    loads[7].wait()
+    send_on(0, 0, 0, 1)
+    finish_pre(0, range(1, steps))
+    loads[8].wait()
     for item in stat_copies:
         item.wait_recv()
     for t in range(1, steps):
@@ -426,18 +445,22 @@
                 grad_out(v)
             finish_back(t, v)
             if t < steps - 1:
-                send_on(t, v)
+                send_on(t, v, 0, 1)
+                if v == 1:
+                    send_on(t - 1, 0, 1, 2)
+                elif t == steps - 2:
+                    send_on(t, 0, 1, 2)
             elif v == 1:
                 grad_in(1)
-    middle(0, 1)
-    middle(1, 1)
+                middle(0, 1)
+                middle(1, 1)
     grad_in(0)
     middle(0, 0)
     middle(1, 0)
     for v in (1, 0):
         for which in (2, 0, 1):
             final(which, v)
-    for item in stat_copies + sq_copies:
+    for item in stat_copies + sq_copies(0) + sq_copies(1):
         item.wait_send()
     for v in range(vs):
         for item in pre_copies[v] + gd_copies(v):
@@ -498,9 +521,9 @@
         V((vs, steps, tok, rank), BF16),
         V((peers, vs, steps, tok, rank), BF16),
         V((steps - 1, vs, tok, wid), BF16),
-        V((tok, 128), F32),
-        V((peers, tok, 128), F32),
-        V((tok, 128), F32),
+        V((vs, tok, 128), F32),
+        V((peers, vs, tok, 128), F32),
+        V((vs, tok, 128), F32),
         V((8, lanes), F32),
         V((max(ndp - 1, 1), 8, lanes), F32),
         V((vs, na, nb, rc, half), BF16),
@@ -515,13 +538,13 @@
         V((na, rc, wid), BF16),
         V((lm, rc, wid), BF16),
         V((hm, rc, wid), BF16),
-        DMA((8,)),
-        DMA((2, peers)),
+        DMA((9,)),
+        DMA((2, vs, peers)),
         DMA((2, max(ndp - 1, 1))),
         DMA((2, vs, peers)),
         DMA((2, vs * steps, peers)),
-        DMA((steps - 1, vs)),
-        DMA((steps - 1, vs)),
+        DMA((steps - 1, vs, 2)),
+        DMA((steps - 1, vs, 2)),
         DMA((vs, pmax)),
         DMA((vs, pmax)),
         DMA((vs * steps, pmax)),

time: 105 us -> 114 us (1.086)
  Pallas kernels: 101 us -> 110 us
    pallas_call x1, Pallas kernels: 101 us -> 110 us  [shards(): pl.pallas_call(functools.partial(kernel, dims), out_shape=(V((vs, rc, wid...]
where the time goes in v3:
time: 114 us
  Pallas kernels  110 us (96%)
  local copies, waits for them, and re-layouts  3.61 us (3%)
    pallas_call x1, Pallas kernels, shards(): pl.pallas_call(functools.partial(kernel, dims), out_shape=(V((vs, rc, wid...  110 us
    unnamed x3, local copies, waits for them, and re-layouts  3.61 us

profile of v3, /device:TPU:0, one launch (start us, length us, event | category | flops | bytes accessed | tf_op | source)
XLA Modules:
  0.0 114.2 jit_solution(7720400207166538632)
XLA Ops:
  0.6 109.9 %shard_map.112 = (f32[2,128,2048]{2,1,0:T(8,128)S(1)}, f32[2,128,2048]{2,1,0:T(8,128)S(1)}, bf16[2,128,2048]{2,1,0:T(8,128)(2,1)S(1)}) custom-call(bf16[3,2,128,2048]{3,2,1,0:T(8,128)(2,1)} %bitcast.18, bf16[2,512,2048]{2,1,0:T(8,128)(2,1)} %bitcast.16, bf16[2,512,2048]{2,1,0:T(8,128)(2,1)} %bitcast.17, f32[2,1,2048]{2,1,0:T(1,128)} %gn_ref.1, ...), custom_call_target="tpu_custom_call" | custom-call | tf_op jit(solution)/shard_map/pallas_call | solution.py:557
  110.5 1.3 %copy.18 = f32[2,1,128,2048]{3,2,1,0:T(8,128)} copy(f32[2,1,128,2048]{3,2,1,0:T(8,128)S(1)} %bitcast.14) | data formatting | bytes 4194304
  111.9 1.3 %copy.19 = f32[2,1,128,2048]{3,2,1,0:T(8,128)} copy(f32[2,1,128,2048]{3,2,1,0:T(8,128)S(1)} %bitcast.13) | data formatting | bytes 4194304
  113.2 1.0 copy.20

commit v4 on v3

--- a/solution.py
+++ b/solution.py
@@ -38,8 +38,8 @@
     na, nb = factors(ndp)
     rc = rank // ndp
     full = wid * nt
-    tile = min(256, wid)
-    rtile = min(256, rank)
+    tile = min(512, wid // 2)
+    rtile = min(512, rank)
     half = wid // 2
     lanes = stl.shape[1]
     new_count, _, seq_count = rew_ref.shape
@@ -420,7 +420,7 @@
         item.wait_recv()
     finish_pre(1, [0])
     finish_back(0, 1)
-    send_on(0, 1, 0, 1)
+    send_on(0, 1, 0, 2)
     loads[5].wait()
     loads[6].wait()
     back_part(0, 0)
@@ -432,7 +432,7 @@
         item.wait_recv()
     finish_pre(0, [0])
     finish_back(0, 0)
-    send_on(0, 0, 0, 1)
+    send_on(0, 0, 0, 2)
     finish_pre(0, range(1, steps))
     loads[8].wait()
     for item in stat_copies:
@@ -445,15 +445,11 @@
                 grad_out(v)
             finish_back(t, v)
             if t < steps - 1:
-                send_on(t, v, 0, 1)
-                if v == 1:
-                    send_on(t - 1, 0, 1, 2)
-                elif t == steps - 2:
-                    send_on(t, 0, 1, 2)
+                send_on(t, v, 0, 2)
             elif v == 1:
                 grad_in(1)
-                middle(0, 1)
-                middle(1, 1)
+    middle(0, 1)
+    middle(1, 1)
     grad_in(0)
     middle(0, 0)
     middle(1, 0)

time: 114 us -> 103 us (0.904)
  Pallas kernels: 110 us -> 98.6 us
    pallas_call x1, Pallas kernels: 110 us -> 98.6 us  [shards(): pl.pallas_call(functools.partial(kernel, dims), out_shape=(V((vs, rc, wid...]
where the time goes in v4:
time: 103 us
  Pallas kernels  98.6 us (96%)
  local copies, waits for them, and re-layouts  3.61 us (4%)
    pallas_call x1, Pallas kernels, shards(): pl.pallas_call(functools.partial(kernel, dims), out_shape=(V((vs, rc, wid...  98.6 us
    unnamed x3, local copies, waits for them, and re-layouts  3.61 us

profile of v4, /device:TPU:0, one launch (start us, length us, event | category | flops | bytes accessed | tf_op | source)
XLA Modules:
  0.0 102.8 jit_solution(17753285049128559747)
XLA Ops:
  0.6 98.6 %shard_map.112 = (f32[2,128,2048]{2,1,0:T(8,128)S(1)}, f32[2,128,2048]{2,1,0:T(8,128)S(1)}, bf16[2,128,2048]{2,1,0:T(8,128)(2,1)S(1)}) custom-call(bf16[3,2,128,2048]{3,2,1,0:T(8,128)(2,1)} %bitcast.18, bf16[2,512,2048]{2,1,0:T(8,128)(2,1)} %bitcast.16, bf16[2,512,2048]{2,1,0:T(8,128)(2,1)} %bitcast.17, f32[2,1,2048]{2,1,0:T(1,128)} %gn_ref.1, ...), custom_call_target="tpu_custom_call" | custom-call | tf_op jit(solution)/shard_map/pallas_call | solution.py:553
  99.2 1.3 %copy.18 = f32[2,1,128,2048]{3,2,1,0:T(8,128)} copy(f32[2,1,128,2048]{3,2,1,0:T(8,128)S(1)} %bitcast.14) | data formatting | bytes 4194304
  100.5 1.3 %copy.19 = f32[2,1,128,2048]{3,2,1,0:T(8,128)} copy(f32[2,1,128,2048]{3,2,1,0:T(8,128)S(1)} %bitcast.13) | data formatting | bytes 4194304
  101.8 1.0 copy.20
